TPU v7x, 32 devices: a whole 2x2x4 slice. The times are simulated.
32 devices in a mesh: rows: 32 (over z, y, x, core).
Axes of the slice: x: 2, y: 2, z: 4, core: 2. Of those that a mesh axis runs over, the one named last changes fastest.
Arguments:
- blocks: float32 [512, 4, 256, 256], P('rows'), may hold values from -0.125 to 0.125
- block_cols: int32 [512, 4], P('rows'), may hold values from 0 to 511, as said below
- live_counts: int32 [512], P('rows'), may hold values from 1 to 4, as said below
- onsite_energy: float32 [131072], P('rows'), may hold values from -2 to 2
- precond: float32 [512, 256, 256], P('rows')
- vectors: float32 [32, 131072], P(None, 'rows'), may hold values from -6 to 6
- prev_vectors: float32 [32, 131072], P(None, 'rows'), may hold values from -6 to 6
- prev_image: float32 [32, 131072], P(None, 'rows'), may hold values from -6 to 6
Outputs:
- correction: float32 [32, 131072], P(None, 'rows')
- reduced: float32 [96, 96], replicated
Inputs may be any that keep to these rules, and one draw needn't show every extreme that they name: block_cols[b, s] = (b + o) mod 512, with the offsets o of one block-row distinct and within 0 to 4; every slot holds a valid block-column. Slots s < live_counts[b] are live, the rest are ignored; some block-row has 4 live slots in every draw.
All inputs are finite; a program needn't handle non-finite values.
Results may differ from a plain program's by a relative error of at most 0.00026.
Values sent between devices are 32-bit elements; how exact they have to be, the bound alone decides.
A program may use at most 128 MiB of HBM per device.

v0:
```python
import functools

import jax
import jax.numpy as jnp
from jax import lax
from jax.experimental import pallas as pl
from jax.experimental.pallas import tpu as pltpu
from jax.sharding import PartitionSpec as P

HB = 4
ITERS = 3
MESH = pl.DeviceIdType.MESH
F32 = jnp.float32
BF16 = jnp.bfloat16
NN = (((1,), (0,)), ((), ()))
NT = (((1,), (1,)), ((), ()))


def split(x):
    high = x.astype(BF16)
    low = (x - high.astype(F32)).astype(BF16)
    return high, low


def dot(a, b, dims):
    return lax.dot_general(a, b, dims, preferred_element_type=F32)


def dot3(pair, high, low, dims):
    rows = pair.shape[0] // 2
    both = dot(pair, high, dims)
    return both[:rows] + both[rows:] + dot(pair[:rows], low, dims)


def kernel(
    n, cols, counts, blocks, precond, onsite, vectors, prev_vectors, prev_image,
    correction, reduced,
    w_high, w_low, m_high, m_low, stage, pstage, field, pair, acc, image, rem, app, hcorr, srch,
    halo_in, land_in, part, sums_in, gp, gp_in, gsum, gall, work,
    load_sem, pload_sem, halo_send, halo_recv, land_send, land_recv,
    sum_send, sum_recv, gp_send, gp_recv, ga_send, ga_recv,
):
    me = lax.axis_index("rows")
    right, left = lax.rem(me + 1, n), lax.rem(me + n - 1, n)
    br, slots, bs = blocks.shape[0], blocks.shape[1], blocks.shape[2]
    kv = vectors.shape[0]
    total = br * n
    first = br - HB

    def lanes(b):
        return pl.ds(pl.multiple_of(b * bs, bs), bs)

    def order(t):
        return lax.rem(t + first, br)

    def load(t):
        b = order(t)
        return pltpu.make_async_copy(blocks.at[b], stage.at[lax.rem(t, 3)], load_sem.at[lax.rem(t, 3)])

    def pload(b):
        return pltpu.make_async_copy(precond.at[b], pstage.at[lax.rem(b, 2)], pload_sem.at[lax.rem(b, 2)])

    load(0).start()
    load(1).start()
    load(2).start()
    pload(0).start()
    pload(1).start()

    barrier = pltpu.get_barrier_semaphore()

    def greet(d, _):
        pl.semaphore_signal(barrier, inc=1, device_id=(lax.rem(me + d, n),), device_id_type=MESH)
        return 0

    lax.fori_loop(1, n, greet, 0)

    def take_vectors(b, _):
        x = vectors[:, lanes(b)]
        field[b] = x
        high, low = split(x)
        pair[b, :kv] = high
        pair[b, kv:] = low
        return 0

    lax.fori_loop(0, br, take_vectors, 0)
    pair[br + HB] = jnp.zeros((2 * kv, bs), BF16)
    pl.semaphore_wait(barrier, n - 1)

    def offset(b, s):
        return lax.rem(cols[b, s] - (me * br + b) + total, total)

    def spread(b):
        moved = dot3(pair[b], w_high[b], w_low[b], NN)
        parts = [moved[:, s * bs:(s + 1) * bs] for s in range(slots)]
        offs = [jnp.where(s < counts[b], offset(b, s), HB + 1) for s in range(slots)]
        for k in range(HB + 1):
            got = acc[b + k]
            for s in range(slots):
                got = got + jnp.where(offs[s] == k, 1.0, 0.0).astype(F32) * parts[s]
            acc[b + k] = got

    def forward(b):
        picks = []
        for s in range(slots):
            at = jnp.where(s < counts[b], b + offset(b, s), br + HB)
            picks.append(pair[at])
        wide = jnp.concatenate(picks, axis=1)
        acc[b] = acc[b] + dot3(wide, w_high[b], w_low[b], NT)

    def take_tiles(t):
        load(t).wait()
        b = order(t)
        for s in range(slots):
            high, low = split(stage[lax.rem(t, 3), s])
            w_high[b, :, s * bs:(s + 1) * bs] = high
            w_low[b, :, s * bs:(s + 1) * bs] = low

        @pl.when(t + 3 < br)
        def _():
            load(t + 3).start()

    def operate(k, loading):
        halo = pltpu.make_async_remote_copy(
            src_ref=field.at[pl.ds(0, HB)], dst_ref=halo_in.at[k],
            send_sem=halo_send.at[k], recv_sem=halo_recv.at[k],
            device_id=(left,), device_id_type=MESH)
        halo.start()

        def clear(b, _):
            acc[b] = jnp.zeros((kv, bs), F32)
            return 0

        lax.fori_loop(0, br + HB, clear, 0)

        def late(t, _):
            if loading:
                take_tiles(t)
            spread(first + t)
            return 0

        lax.fori_loop(0, HB, late, 0, unroll=1 if loading else 2)
        land = pltpu.make_async_remote_copy(
            src_ref=acc.at[pl.ds(br, HB)], dst_ref=land_in.at[k],
            send_sem=land_send.at[k], recv_sem=land_recv.at[k],
            device_id=(right,), device_id_type=MESH)
        land.start()

        def main(b, _):
            if loading:
                take_tiles(b + HB)
            spread(b)
            if not loading:
                forward(b)
            return 0

        lax.fori_loop(0, first, main, 0, unroll=1 if loading else 2)
        if loading:
            def again(b, _):
                forward(b)
                return 0

            lax.fori_loop(0, first, again, 0, unroll=2)
        halo.wait_recv()

        def take_halo(i, _):
            high, low = split(halo_in[k, i])
            pair[br + i, :kv] = high
            pair[br + i, kv:] = low
            return 0

        lax.fori_loop(0, HB, take_halo, 0)

        def tail(b, _):
            forward(b)
            return 0

        lax.fori_loop(first, br, tail, 0, unroll=2)
        land.wait_recv()

        def take_land(i, _):
            acc[i] = acc[i] + land_in[k, i]
            return 0

        lax.fori_loop(0, HB, take_land, 0)
        halo.wait_send()
        land.wait_send()

    def sum_copy(k, d):
        return pltpu.make_async_remote_copy(
            src_ref=part.at[k], dst_ref=sums_in.at[k, me],
            send_sem=sum_send.at[k, d], recv_sem=sum_recv.at[k, me],
            device_id=(lax.rem(me + d, n),), device_id_type=MESH)

    def sum_start(k, one, two):
        folded = jnp.concatenate([one, two], axis=0)
        folded = folded[:, :128] + folded[:, 128:]
        wide = jnp.broadcast_to(jnp.sum(folded, axis=1, keepdims=True), (2 * kv, 128))
        wide = jnp.concatenate([wide, jnp.zeros((128 - 2 * kv, 128), F32)], axis=0)
        mine = wide.T[:8]
        part[k] = mine
        sums_in[k, me] = mine

        def send(d, _):
            sum_copy(k, d).start()
            return 0

        lax.fori_loop(1, n, send, 0)

    def sum_finish(k):
        def arrive(d, _):
            who = lax.rem(me + d, n)
            pltpu.make_async_remote_copy(
                src_ref=part.at[k], dst_ref=sums_in.at[k, who],
                send_sem=sum_send.at[k, d], recv_sem=sum_recv.at[k, who],
                device_id=(who,), device_id_type=MESH).wait_recv()
            return 0

        lax.fori_loop(1, n, arrive, 0)

        def add(i, so_far):
            return so_far + sums_in[k, i]

        whole = lax.fori_loop(0, n, add, jnp.zeros((8, 128), F32))

        def sent(d, _):
            sum_copy(k, d).wait_send()
            return 0

        lax.fori_loop(1, n, sent, 0)
        column = jnp.broadcast_to(whole[0:1], (128, 128)).T
        column = jnp.concatenate([column, column], axis=1)
        return column[:kv], column[kv:2 * kv]

    zero = jnp.zeros((kv, bs), F32)
    operate(0, True)

    def rayleigh(b, sums):
        x = vectors[:, lanes(b)]
        y = acc[b] + onsite[:, lanes(b)] * x
        image[b] = y
        return sums[0] + x * y, sums[1] + x * x

    sum_start(0, *lax.fori_loop(0, br, rayleigh, (zero, zero)))

    def take_precond(b, _):
        pload(b).wait()
        high, low = split(pstage[lax.rem(b, 2)])
        m_high[b] = high
        m_low[b] = low

        @pl.when(b + 2 < br)
        def _():
            pload(b + 2).start()
        correction[:, lanes(b)] = zero
        hcorr[b] = zero
        return 0

    lax.fori_loop(0, br, take_precond, 0)
    numerator, denominator = sum_finish(0)
    quotient = numerator / denominator

    def begin(b, _):
        rem[b] = quotient * vectors[:, lanes(b)] - image[b]
        return 0

    lax.fori_loop(0, br, begin, 0)

    def precondition(source):
        def body(b, _):
            high, low = split(source[b])
            x = dot3(jnp.concatenate([high, low], axis=0), m_high[b], m_low[b], NT)
            field[b] = x
            high, low = split(x)
            pair[b, :kv] = high
            pair[b, kv:] = low
            return 0

        lax.fori_loop(0, br, body, 0, unroll=4)

    precondition(rem)
    operate(1, False)

    def apply(b, sums):
        x = field[b]
        y = acc[b] + (onsite[:, lanes(b)] - quotient) * x
        srch[b] = x
        app[b] = y
        return sums[0] + y * rem[b], sums[1] + y * y

    sum_start(1, *lax.fori_loop(0, br, apply, (zero, zero)))
    for it in range(ITERS):
        last = it == ITERS - 1
        if not last:
            precondition(app)
            operate(it + 2, False)
        cross, own = sum_finish(it + 1)
        step = cross / (own + 1.0)

        def update(b, sums):
            x, y = srch[b], app[b]
            correction[:, lanes(b)] = correction[:, lanes(b)] + step * x
            hcorr[b] = hcorr[b] + step * (y + quotient * x)
            if last:
                return sums
            turned = field[b]
            r = rem[b] - step * y
            z = y - step * (acc[b] + (onsite[:, lanes(b)] - quotient) * turned)
            srch[b] = x - step * turned
            rem[b] = r
            app[b] = z
            return sums[0] + z * r, sums[1] + z * z

        sums = lax.fori_loop(0, br, update, (zero, zero), unroll=2)
        if not last:
            sum_start(it + 2, *sums)

    nb = 3 * kv

    def gram(b, so_far):
        basis = jnp.concatenate(
            [vectors[:, lanes(b)], prev_vectors[:, lanes(b)], correction[:, lanes(b)]], axis=0)
        other = jnp.concatenate([image[b], prev_image[:, lanes(b)], hcorr[b]], axis=0)
        bh, bl = split(basis)
        oh, ol = split(other)
        high = jnp.concatenate([bh, oh], axis=0)
        low = jnp.concatenate([bl, ol], axis=0)
        return so_far + dot(bh, high, NT) + dot(bl, high, NT) + dot(bh, low, NT)

    both = lax.fori_loop(0, br, gram, jnp.zeros((nb, 2 * nb), F32), unroll=2)
    pad = jnp.zeros((nb, 128 - nb), F32)
    sheet = jnp.concatenate(
        [jnp.concatenate([both[:, :nb], pad], axis=1), jnp.concatenate([both[:, nb:], pad], axis=1)],
        axis=0)
    chunks = 2 * nb // 8
    for c in range(chunks):
        gp[c] = sheet[c * 8:(c + 1) * 8]

    def scatter(d):
        to = lax.rem(me + d, n)
        return to, pltpu.make_async_remote_copy(
            src_ref=gp.at[jnp.minimum(to, chunks - 1)], dst_ref=gp_in.at[me],
            send_sem=gp_send.at[d], recv_sem=gp_recv.at[me],
            device_id=(to,), device_id_type=MESH)

    def scatter_send(d, _):
        to, copy = scatter(d)

        @pl.when(to < chunks)
        def _():
            copy.start()
        return 0

    lax.fori_loop(1, n, scatter_send, 0)

    def gather(d):
        to = lax.rem(me + d, n)
        return pltpu.make_async_remote_copy(
            src_ref=gsum, dst_ref=gall.at[me],
            send_sem=ga_send.at[d], recv_sem=ga_recv.at[me],
            device_id=(to,), device_id_type=MESH)

    @pl.when(me < chunks)
    def _():
        gp_in[me] = gp[me]

        def arrive(d, _):
            who = lax.rem(me + d, n)
            pltpu.make_async_remote_copy(
                src_ref=gsum, dst_ref=gp_in.at[who],
                send_sem=gp_send.at[d], recv_sem=gp_recv.at[who],
                device_id=(who,), device_id_type=MESH).wait_recv()
            return 0

        lax.fori_loop(1, n, arrive, 0)

        def add(i, so_far):
            return so_far + gp_in[i]

        mine = lax.fori_loop(0, n, add, jnp.zeros((8, 128), F32))
        gsum[...] = mine
        gall[me] = mine

        def send(d, _):
            gather(d).start()
            return 0

        lax.fori_loop(1, n, send, 0)

    def gathered(c, _):
        @pl.when(c != me)
        def _():
            pltpu.make_async_remote_copy(
                src_ref=gsum, dst_ref=gall.at[c],
                send_sem=ga_send.at[0], recv_sem=ga_recv.at[c],
                device_id=(right,), device_id_type=MESH).wait_recv()
        return 0

    lax.fori_loop(0, chunks, gathered, 0)

    def scatter_done(d, _):
        to, copy = scatter(d)

        @pl.when(to < chunks)
        def _():
            copy.wait_send()

        @pl.when(me < chunks)
        def _():
            gather(d).wait_send()
        return 0

    lax.fori_loop(1, n, scatter_done, 0)

    rows_at = lax.broadcasted_iota(jnp.int32, (nb, 128), 0)
    cols_at = lax.broadcasted_iota(jnp.int32, (nb, 128), 1)
    eye = jnp.where(rows_at == cols_at, 1.0, 0.0).astype(F32)
    half = chunks // 2
    g = jnp.concatenate([gall[c] for c in range(half)], axis=0)
    p = jnp.concatenate([gall[half + c] for c in range(half)], axis=0)
    work[:, 0:128] = g + eye
    work[:, 128:256] = p
    work[:, 256:384] = eye

    def eliminate(j, _):
        column = jnp.sum(jnp.where(cols_at == j, work[:, 0:128], 0.0), axis=1, keepdims=True)
        row = work[pl.ds(j, 1), :]
        pivot = jnp.sum(jnp.where(lane_at == j, row[:, :128], 0.0), axis=1, keepdims=True)
        below = jnp.where(rows_at[:, 0:1] > j, column / pivot, 0.0)
        work[...] = work[...] - below * row
        return 0

    lane_at = lax.broadcasted_iota(jnp.int32, (1, 128), 1)
    lax.fori_loop(0, nb, eliminate, 0, unroll=2)
    diagonal = jnp.sum(jnp.where(rows_at == cols_at, work[:, 0:128], 0.0), axis=1, keepdims=True)
    scale = 1.0 / jnp.sqrt(diagonal)
    half_way = scale * work[:, 128:256]
    inverse = scale * work[:, 256:384]
    answer = lax.dot_general(
        half_way[:, :nb], inverse[:, :nb], NT, precision=lax.Precision.HIGHEST,
        preferred_element_type=F32)
    reduced[...] = answer


def local(blocks, block_cols, live_counts, onsite_energy, precond, vectors, prev_vectors, prev_image):
    n = lax.axis_size("rows")
    br, slots, bs, _ = blocks.shape
    kv, width = vectors.shape
    nb = 3 * kv
    vmem = pl.BlockSpec(memory_space=pltpu.VMEM)
    smem = pl.BlockSpec(memory_space=pltpu.SMEM)
    hbm = pl.BlockSpec(memory_space=pl.ANY)
    dma = pltpu.SemaphoreType.DMA
    rounds = ITERS + 1
    chunks = 2 * nb // 8
    return pl.pallas_call(
        functools.partial(kernel, n),
        out_shape=(
            jax.ShapeDtypeStruct((kv, width), F32),
            jax.ShapeDtypeStruct((nb, nb), F32),
        ),
        in_specs=[smem, smem, hbm, hbm, vmem, vmem, vmem, vmem],
        out_specs=(vmem, vmem),
        scratch_shapes=[
            pltpu.VMEM((br, bs, slots * bs), BF16),
            pltpu.VMEM((br, bs, slots * bs), BF16),
            pltpu.VMEM((br, bs, bs), BF16),
            pltpu.VMEM((br, bs, bs), BF16),
            pltpu.VMEM((3, slots, bs, bs), F32),
            pltpu.VMEM((2, bs, bs), F32),
            pltpu.VMEM((br, kv, bs), F32),
            pltpu.VMEM((br + HB + 1, 2 * kv, bs), BF16),
            pltpu.VMEM((br + HB, kv, bs), F32),
            pltpu.VMEM((br, kv, bs), F32),
            pltpu.VMEM((br, kv, bs), F32),
            pltpu.VMEM((br, kv, bs), F32),
            pltpu.VMEM((br, kv, bs), F32),
            pltpu.VMEM((br, kv, bs), F32),
            pltpu.VMEM((rounds, HB, kv, bs), F32),
            pltpu.VMEM((rounds, HB, kv, bs), F32),
            pltpu.VMEM((rounds, 8, 128), F32),
            pltpu.VMEM((rounds, n, 8, 128), F32),
            pltpu.VMEM((chunks, 8, 128), F32),
            pltpu.VMEM((n, 8, 128), F32),
            pltpu.VMEM((8, 128), F32),
            pltpu.VMEM((chunks, 8, 128), F32),
            pltpu.VMEM((nb, 384), F32),
            dma((3,)),
            dma((2,)),
            dma((rounds,)),
            dma((rounds,)),
            dma((rounds,)),
            dma((rounds,)),
            dma((rounds, n)),
            dma((rounds, n)),
            dma((n,)),
            dma((n,)),
            dma((n,)),
            dma((n,)),
        ],
        compiler_params=pltpu.CompilerParams(
            collective_id=0, has_side_effects=True, vmem_limit_bytes=60 * 1024 * 1024
        ),
    )(block_cols, live_counts, blocks, precond, onsite_energy[None, :], vectors, prev_vectors, prev_image)


def solution(mesh):
    placed = (
        P("rows", None, None, None),
        P("rows", None),
        P("rows"),
        P("rows"),
        P("rows", None, None),
        P(None, "rows"),
        P(None, "rows"),
        P(None, "rows"),
    )
    return jax.shard_map(
        local, mesh=mesh, in_specs=placed, out_specs=(P(None, "rows"), P()), check_vma=False
    )
```

profile of v0, /device:TPU:25, one launch (start us, length us, event | category | flops | bytes accessed | tf_op | source)
XLA Modules:
  0.0 105.0 jit_solution(8896023498955975744)
XLA Ops:
  0.6 1.4 %copy.10.cols = s32[16,4]{1,0:T(8,128)} copy(s32[16,4]{0,1:T(4,128)} %param.9) | data formatting | bytes 512 | tf_op args[1]
  2.0 99.7 %shard_map.95 = (f32[32,4096]{1,0:T(8,128)}, f32[96,96]{1,0:T(8,128)}) custom-call(s32[16,4]{1,0:T(8,128)} %copy.10.cols, s32[16]{0:T(128)} %counts.1, f32[16,4,256,256]{3,2,1,0:T(8,128)} %blocks.1, f32[16,256,256]{2,1,0:T(8,128)} %precond.1, f32[1,4096]{1,0:T(1,128)} %bitcast.1, f32[32,4096]{1,0:T(8,128)} %vectors.1, f32[32,4096]{1,0:T(8,128)} %prev_vectors.1, ...), custom_call_target="tpu_custom_call" | custom-call | tf_op jit(solution)/shard_map/pallas_call | solution.py:455
  101.7 1.9 %copy.13 = f32[32,4096]{1,0:T(8,128)} copy(f32[32,4096]{1,0:T(8,128)} %get-tuple-element.4) | data formatting | bytes 1048576
  103.5 1.4 %copy.14 = f32[96,96]{1,0:T(8,128)} copy(f32[96,96]{1,0:T(8,128)} %get-tuple-element.5) | data formatting | bytes 73728
where the time goes:
time: 107 us; the launch traced here: 105 us
  Pallas kernels  99.7 us (93%)
  local copies, waits for them, and re-layouts  4.65 us (4%)
    pallas_call x1, Pallas kernels, local(): pl.pallas_call(functools.partial(kernel, n), out_shape=(jax.ShapeDtypeStr...  99.7 us
    unnamed x3, local copies, waits for them, and re-layouts  4.65 us

commit v1 on v0

v1 whole, which is shorter than its diff:
```python
import functools

import jax
import jax.numpy as jnp
from jax import lax
from jax.experimental import pallas as pl
from jax.experimental.pallas import tpu as pltpu
from jax.sharding import PartitionSpec as P

HB = 4
MESH = pl.DeviceIdType.MESH
F32 = jnp.float32
BF16 = jnp.bfloat16
E4M3 = jnp.float8_e4m3fn
NN = (((1,), (0,)), ((), ()))
NT = (((1,), (1,)), ((), ()))
LOW = 2.0 ** 20
RING = 8
ROUNDS = 3


def dot(a, b, dims):
    return lax.dot_general(a, b, dims, preferred_element_type=F32)


def hdot(a, b, dims):
    return lax.dot_general(a, b, dims, precision=lax.Precision.HIGHEST, preferred_element_type=F32)


def split(x):
    high = x.astype(BF16)
    low = (x - high.astype(F32)).astype(BF16)
    return high, low


def factor_inverse(s):
    m = s.shape[0]
    rows = lax.broadcasted_iota(jnp.int32, (m, 128), 0)
    lanes = lax.broadcasted_iota(jnp.int32, (m, m), 1)
    eye = jnp.where(lanes == lax.broadcasted_iota(jnp.int32, (m, m), 0), 1.0, 0.0).astype(F32)
    work = jnp.concatenate([s, eye, jnp.zeros((m, 128 - 2 * m), F32)], axis=1)
    diagonal = jnp.ones((m, 128), F32)
    for first in range(0, m, 8):
        column = [jnp.broadcast_to(work[:, first + i:first + i + 1], (m, 128)) for i in range(8)]
        for i in range(8):
            j = first + i
            pivot = column[i][j:j + 1]
            diagonal = jnp.where(rows == j, column[i], diagonal)
            below = jnp.where(rows > j, column[i] * (1.0 / pivot), 0.0)
            work = work - below * work[j:j + 1]
            for k in range(i + 1, 8):
                column[k] = column[k] - below * column[k][j:j + 1]
    return (work / jnp.sqrt(diagonal))[:, m:2 * m]


def kernel(
    n, cols, counts, blocks, precond, onsite_hbm, vectors_hbm, prev_vectors_hbm, prev_image_hbm,
    correction, reduced,
    w_high, w_low, t_high, t_low, m_high, m_low, stage, pstage,
    onsite, vec, pvec, pimg, cor,
    field, fieldv, pair, pairv, moved, movedv, fwd, fwdv,
    image, rem, app, hcorr, srch,
    halo_in, halov_in, land_out, land_in, landv_out, landv_in,
    part, sums_in, e_part, e_in, e_sum, e_all, l_part, l_in, l_sum, l_all, early,
    load_sem, pload_sem, in_sem, out_sem, halo_send, halo_recv, land_send, land_recv,
    sum_send, sum_recv, r_send, r_recv, a_send, a_recv,
):
    me = lax.axis_index("rows")
    right, left = lax.rem(me + 1, n), lax.rem(me + n - 1, n)
    br, slots, bs = blocks.shape[0], blocks.shape[1], blocks.shape[2]
    kv = 32
    total = br * n
    first = br - HB
    order = list(range(first, br)) + list(range(first))
    pchunk = br // 4

    def lanes(b):
        return pl.ds(b * bs, bs)

    def load(t):
        return pltpu.make_async_copy(blocks.at[order[t]], stage.at[t % RING], load_sem.at[t])

    def pload(c):
        at = pl.ds(c * pchunk, pchunk)
        return pltpu.make_async_copy(precond.at[at], pstage.at[at], pload_sem.at[c])

    inputs = [
        pltpu.make_async_copy(vectors_hbm, vec, in_sem.at[0]),
        pltpu.make_async_copy(onsite_hbm, onsite, in_sem.at[1]),
        pltpu.make_async_copy(prev_vectors_hbm, pvec, in_sem.at[2]),
        pltpu.make_async_copy(prev_image_hbm, pimg, in_sem.at[3]),
    ]
    barrier = pltpu.get_barrier_semaphore()
    inputs[0].start()
    inputs[1].start()
    for t in range(RING):
        load(t).start()

    def greet(d, _):
        pl.semaphore_signal(barrier, inc=1, device_id=(lax.rem(me + d, n),), device_id_type=MESH)
        return 0

    lax.fori_loop(1, n, greet, 0)

    def offset(b, s):
        return lax.rem(cols[s, b] - (me * br + b) + total, total)

    def source(b, s):
        return jnp.where(s < counts[b], b + offset(b, s), br + HB)

    def slot_of(b, k):
        at = jnp.int32(slots)
        for s in range(slots):
            at = jnp.where((s < counts[b]) & (offset(b, s) == k), s, at)
        return at

    def put(to, b, x):
        high = x.astype(BF16)
        wide = high.astype(F32)
        to[b, 0:kv] = high
        to[b, kv:2 * kv] = (x - wide).astype(BF16)
        to[b, 2 * kv:3 * kv] = (wide * (1.0 / LOW)).astype(BF16)

    def take_tiles(t):
        b = order[t]
        for s in range(slots):
            at = slice(s * bs, (s + 1) * bs)
            x = stage[t % RING, s]
            high = x.astype(BF16)
            low = ((x - high.astype(F32)) * LOW).astype(E4M3)
            w_high[b, :, at] = high
            w_low[b, :, at] = low
            t_high[b, at, :] = high.T
            t_low[b, at, :] = low.T

    def spread(b, groups):
        lhs = jnp.concatenate([g[0][b, 0:2 * kv] for g in groups], axis=0)
        out = dot(lhs, w_high[b], NN)
        low = dot(jnp.concatenate([g[0][b, 2 * kv:3 * kv] for g in groups], axis=0), w_low[b], NN)
        for i, g in enumerate(groups):
            whole = out[2 * i * kv:(2 * i + 1) * kv] + out[(2 * i + 1) * kv:(2 * i + 2) * kv] + low[i * kv:(i + 1) * kv]
            for s in range(slots):
                g[1][b, s] = whole[:, s * bs:(s + 1) * bs]

    def forward(b, groups):
        at = [source(b, s) for s in range(slots)]
        lhs = jnp.concatenate(
            [jnp.concatenate([g[0][a, 0:2 * kv] for a in at], axis=1) for g in groups], axis=0)
        lhs_low = jnp.concatenate(
            [jnp.concatenate([g[0][a, 2 * kv:3 * kv] for a in at], axis=1) for g in groups], axis=0)
        out = dot(lhs, t_high[b], NN)
        low = dot(lhs_low, t_low[b], NN)
        for i, g in enumerate(groups):
            g[2][b] = out[2 * i * kv:(2 * i + 1) * kv] + out[(2 * i + 1) * kv:(2 * i + 2) * kv] + low[i * kv:(i + 1) * kv]

    def landing(group, b):
        got = None
        for k in range(HB + 1):
            c = b - k
            if 0 <= c < br:
                one = group[1][c, slot_of(c, k)]
                got = one if got is None else got + one
        return got

    def halo_copy(k, src, dst):
        return pltpu.make_async_remote_copy(
            src_ref=src.at[pl.ds(0, HB)], dst_ref=dst,
            send_sem=halo_send.at[k], recv_sem=halo_recv.at[k],
            device_id=(left,), device_id_type=MESH)

    def land_copy(k, src, dst):
        return pltpu.make_async_remote_copy(
            src_ref=src, dst_ref=dst,
            send_sem=land_send.at[k], recv_sem=land_recv.at[k],
            device_id=(right,), device_id_type=MESH)

    main = (pair, moved, fwd)
    side = (pairv, movedv, fwdv)

    def blockloop(lo, hi, body, unroll):
        def step(b, _):
            body(b)
            return 0

        lax.fori_loop(lo, hi, step, 0, unroll=unroll)

    def precondition(b, x):
        high, low = split(x)
        both = dot(jnp.concatenate([high, low], axis=0), m_high[b], NN)
        return both[:kv] + both[kv:] + dot(high, m_low[b], NN)

    def sum_copy(k, d):
        return pltpu.make_async_remote_copy(
            src_ref=part.at[k], dst_ref=sums_in.at[k, me],
            send_sem=sum_send.at[k], recv_sem=sum_recv.at[k],
            device_id=(lax.rem(me + d, n),), device_id_type=MESH)

    def lane_sums(one, two):
        folded = jnp.concatenate([one, two], axis=0)
        folded = folded[:, :128] + folded[:, 128:]
        return jnp.sum(folded, axis=1, keepdims=True)

    def sum_start(k, one, two):
        wide = jnp.broadcast_to(lane_sums(one, two), (2 * kv, 128))
        wide = jnp.concatenate([wide, jnp.zeros((128 - 2 * kv, 128), F32)], axis=0)
        mine = wide.T[:1]
        part[k] = mine
        sums_in[k, me] = mine

        def send(d, _):
            sum_copy(k, d).start()
            return 0

        lax.fori_loop(1, n, send, 0)

    def bulk(ref, sem):
        return pltpu.make_async_copy(ref, ref, sem)

    def sum_finish(k):
        bulk(sums_in.at[k, pl.ds(0, n - 1)], sum_recv.at[k]).wait()
        whole = jnp.sum(sums_in[k], axis=0)
        bulk(sums_in.at[k, pl.ds(0, n - 1)], sum_send.at[k]).wait()
        column = jnp.broadcast_to(whole, (128, 128)).T
        column = jnp.concatenate([column, column], axis=1)
        return column[:kv], column[kv:2 * kv]

    def scatter(r, sheet, held, landed):
        chunks = held.shape[0]
        for c in range(chunks):
            held[c] = sheet[c]

        def send(d, _):
            to = lax.rem(me + d, n)

            @pl.when(to < chunks)
            def _():
                pltpu.make_async_remote_copy(
                    src_ref=held.at[jnp.minimum(to, chunks - 1)], dst_ref=landed.at[me],
                    send_sem=r_send.at[r], recv_sem=r_recv.at[r],
                    device_id=(to,), device_id_type=MESH).start()
            return 0

        lax.fori_loop(1, n, send, 0)

    def spread_sums(r, held, landed, mine, everything):
        chunks = held.shape[0]

        @pl.when(me < chunks)
        def _():
            bulk(landed.at[pl.ds(0, n - 1)], r_recv.at[r]).wait()
            landed[me] = held[jnp.minimum(me, chunks - 1)]
            whole = jnp.sum(landed[...], axis=0)
            mine[...] = whole
            everything[jnp.minimum(me, chunks - 1)] = whole

            def send(d, _):
                pltpu.make_async_remote_copy(
                    src_ref=mine, dst_ref=everything.at[jnp.minimum(me, chunks - 1)],
                    send_sem=a_send.at[r], recv_sem=a_recv.at[r],
                    device_id=(lax.rem(me + d, n),), device_id_type=MESH).start()
                return 0

            lax.fori_loop(1, n, send, 0)

    def collect(r, held, landed, everything):
        chunks = held.shape[0]

        @pl.when(me < chunks)
        def _():
            bulk(everything.at[pl.ds(0, chunks - 1)], a_recv.at[r]).wait()

        @pl.when(me >= chunks)
        def _():
            bulk(everything, a_recv.at[r]).wait()

    def drain(r, held, landed):
        chunks = held.shape[0]

        @pl.when(me < chunks)
        def _():
            bulk(held.at[pl.ds(0, chunks - 1)], r_send.at[r]).wait()
            bulk(landed.at[pl.ds(0, n - 1)], a_send.at[r]).wait()

        @pl.when(me >= chunks)
        def _():
            bulk(held, r_send.at[r]).wait()

    zero = jnp.zeros((kv, bs), F32)
    for c in range(br):
        moved[c, slots] = zero
        movedv[c, slots] = zero
    pair[br + HB] = jnp.zeros((3 * kv, bs), BF16)
    pairv[br + HB] = jnp.zeros((3 * kv, bs), BF16)
    inputs[0].wait()
    for b in range(br):
        x = vec[:, lanes(b)]
        put(pair, b, x)
        if b < HB:
            field[b] = x

    def advance(t):
        load(t).wait()
        take_tiles(t)
        if t + RING < br:
            load(t + RING).start()
        elif t + RING == br:
            for c in range(4):
                pload(c).start()
            inputs[2].start()
            inputs[3].start()

    for t in range(HB):
        advance(t)
        spread(order[t], [main])
    for i in range(HB):
        land_out[i] = landing(main, br + i)
    pl.semaphore_wait(barrier, n - 1)
    halo = halo_copy(0, field, halo_in.at[0])
    halo.start()
    land = land_copy(0, land_out, land_in.at[0])
    land.start()
    for t in range(HB, br):
        advance(t)
        spread(order[t], [main])
        if t - HB >= HB:
            forward(t - 2 * HB, [main])
    for b in range(first - HB, first):
        forward(b, [main])

    for c in range(4):
        pload(c).wait()
    for b in range(br):
        high, low = split(pstage[b])
        m_high[b] = high.T
        m_low[b] = low.T

    def side_block(b):
        x = precondition(b, vec[:, lanes(b)])
        fieldv[b] = x
        put(pairv, b, x)

    for b in list(range(HB)) + list(range(first, br)):
        side_block(b)
    halov = halo_copy(4, fieldv, halov_in)
    halov.start()
    for b in range(first, br):
        spread(b, [side])
    for i in range(HB):
        landv_out[i] = landing(side, br + i)
    landv = land_copy(4, landv_out, landv_in)
    landv.start()
    for b in range(HB, first):
        side_block(b)

    inputs[1].wait()

    def finish(k, groups, halo, land, more):
        halo.wait_recv()
        for i in range(HB):
            put(pair, br + i, halo_in[k, i])
        if more:
            more[0].wait_recv()
            for i in range(HB):
                put(pairv, br + i, halov_in[i])
        for b in range(first, br):
            forward(b, groups)
        land.wait_recv()
        if more:
            more[1].wait_recv()
        for copy in (halo, land) + tuple(more):
            copy.wait_send()

    def applied(k, group, landed, held, b):
        got = group[2][b] + landing(group, b) + onsite[:, lanes(b)] * held[b]
        return got + landed(b) if b < HB else got

    def middle(k, update, groups):
        sums = [zero, zero]

        def one(b):
            out, a, c = update(b)
            sums[0] = sums[0] + a
            sums[1] = sums[1] + c
            return out

        def pre(b, x):
            y = precondition(b, x)
            field[b] = y
            put(pair, b, y)

        for b in range(HB):
            pre(b, one(b))
        halo = halo_copy(k, field, halo_in.at[k])
        halo.start()
        outs = [one(b) for b in range(first, br)]
        for b in range(first, br):
            pre(b, outs[b - first])
        for b in range(first, br):
            spread(b, [main])
        for i in range(HB):
            land_out[i] = landing(main, br + i)
        land = land_copy(k, land_out, land_in.at[k])
        land.start()
        outs = [one(b) for b in range(HB, first)]
        sum_start(k - 1, *sums)
        for b in range(HB, first):
            pre(b, outs[b - HB])
        blockloop(0, first, lambda b: spread(b, groups), 4)
        blockloop(0, first, lambda b: forward(b, groups), 4)
        return halo, land

    finish(0, [main], halo, land, ())

    def after0(b):
        x = vec[:, lanes(b)]
        got = fwd[b] + landing(main, b) + onsite[:, lanes(b)] * x
        if b < HB:
            got = got + land_in[0, b]
        image[b] = got
        return got, x * got, x * x

    halo, land = middle(1, after0, [main, side])
    inputs[2].wait()
    inputs[3].wait()
    both = jnp.zeros((2 * kv, 4 * kv), F32)
    for b in range(br):
        basis = jnp.concatenate([vec[:, lanes(b)], pvec[:, lanes(b)]], axis=0)
        other = jnp.concatenate([basis, image[b], pimg[:, lanes(b)]], axis=0)
        oh, ol = split(other)
        bh, bl = oh[:2 * kv], ol[:2 * kv]
        both = both + dot(bh, oh, NT) + dot(bl, oh, NT) + dot(bh, ol, NT)
    scatter(0, [both[c * 8:(c + 1) * 8] for c in range(8)], e_part, e_in)
    finish(1, [main, side], halo, land, (halov, landv))
    numerator, denominator = sum_finish(0)
    quotient = numerator / denominator

    def after1(b):
        xv, xi = fieldv[b], field[b]
        on = onsite[:, lanes(b)]
        hv = fwdv[b] + landing(side, b) + on * xv
        hi = fwd[b] + landing(main, b) + on * xi
        if b < HB:
            hv = hv + landv_in[b]
            hi = hi + land_in[1, b]
        x = quotient * xv - xi
        r = quotient * vec[:, lanes(b)] - image[b]
        a = quotient * hv - hi - quotient * x
        srch[b] = x
        rem[b] = r
        app[b] = a
        return a, a * r, a * a

    halo, land = middle(2, after1, [main])
    spread_sums(0, e_part, e_in, e_sum, e_all)
    finish(2, [main], halo, land, ())
    step = sum_finish(1)
    step = step[0] / (step[1] + 1.0)

    def advance_step(k, start, b):
        x, y, t = srch[b], app[b], field[b]
        on = onsite[:, lanes(b)]
        g = fwd[b] + landing(main, b) + (on - quotient) * t
        if b < HB:
            g = g + land_in[k, b]
        c = step * x
        h = step * (y + quotient * x)
        cor[:, lanes(b)] = c if start else cor[:, lanes(b)] + c
        hcorr[b] = h if start else hcorr[b] + h
        r = rem[b] - step * y
        z = y - step * g
        srch[b] = x - step * t
        rem[b] = r
        app[b] = z
        return z, z * r, z * z

    halo, land = middle(3, lambda b: advance_step(2, True, b), [main])
    collect(0, e_part, e_in, e_all)
    known = jnp.concatenate([e_all[c] for c in range(8)], axis=0)
    rows_at = lax.broadcasted_iota(jnp.int32, (kv, kv), 0)
    eye = jnp.where(rows_at == lax.broadcasted_iota(jnp.int32, (kv, kv), 1), 1.0, 0.0).astype(F32)
    x11 = factor_inverse(known[:kv, :kv] + eye)
    y21 = hdot(known[kv:2 * kv, :kv], x11, NT)
    x22 = factor_inverse(known[kv:2 * kv, kv:2 * kv] + eye - hdot(y21, y21, NT))
    x21 = -hdot(x22, hdot(y21, x11, NN), NN)
    early[0:kv] = jnp.concatenate([x11, jnp.zeros((kv, 128 - kv), F32)], axis=1)
    early[kv:2 * kv] = jnp.concatenate([x21, x22, jnp.zeros((kv, 128 - 2 * kv), F32)], axis=1)
    finish(3, [main], halo, land, ())
    step = sum_finish(2)
    step = step[0] / (step[1] + 1.0)

    sums = [zero, zero]
    both = jnp.zeros((4 * kv, 8 * kv), F32)
    for b in range(br):
        z, one, two = advance_step(3, False, b)
        sums = [sums[0] + one, sums[1] + two]
        x = srch[b]
        mine = cor[:, lanes(b)]
        hmine = hcorr[b]
        w = z + quotient * x
        ch, cl = split(jnp.concatenate([mine, x], axis=0))
        hh, hl = split(jnp.concatenate([hmine, w], axis=0))
        vh, vl = split(jnp.concatenate([vec[:, lanes(b)], pvec[:, lanes(b)]], axis=0))
        ih, il = split(jnp.concatenate([image[b], pimg[:, lanes(b)]], axis=0))
        lh = jnp.concatenate([ch, hh], axis=0)
        ll = jnp.concatenate([cl, hl], axis=0)
        oh = jnp.concatenate([vh, ch, ih, hh], axis=0)
        ol = jnp.concatenate([vl, cl, il, hl], axis=0)
        both = both + dot(lh, oh, NT) + dot(ll, oh, NT) + dot(lh, ol, NT)
    lane_at = lax.broadcasted_iota(jnp.int32, (2 * kv, 128), 1)
    third = jnp.where(
        lane_at < 2 * kv, both[2 * kv:, :128], jnp.broadcast_to(lane_sums(*sums), (2 * kv, 128)))
    sheets = [both[:2 * kv, :128], both[:2 * kv, 128:], third]
    scatter(1, [s[c * 8:(c + 1) * 8] for s in sheets for c in range(8)], l_part, l_in)
    spread_sums(1, l_part, l_in, l_sum, l_all)
    collect(1, l_part, l_in, l_all)
    one, two, three = [
        jnp.concatenate([l_all[8 * i + c] for c in range(8)], axis=0) for i in range(3)]
    cross = jnp.broadcast_to(three[:kv, 2 * kv:2 * kv + 1], (kv, 128))
    own = jnp.broadcast_to(three[kv:, 2 * kv:2 * kv + 1], (kv, 128))
    step = cross / (own + 1.0)
    wide = jnp.concatenate([step, step], axis=1)
    for b in range(br):
        cor[:, lanes(b)] = cor[:, lanes(b)] + wide * srch[b]
    result = pltpu.make_async_copy(cor, correction, out_sem.at[0])
    result.start()
    row = jnp.concatenate([step, jnp.zeros((128 - kv, 128), F32)], axis=0).T[:kv, :kv]
    one = one[:kv] + step * one[kv:]
    two = two[:kv] + step * two[kv:]
    three = three[:kv] + step * three[kv:]
    gc = one[:, :2 * kv]
    gcc = one[:, 2 * kv:3 * kv] + one[:, 3 * kv:] * row
    pc = two[:, :2 * kv]
    pcc = two[:, 2 * kv:3 * kv] + two[:, 3 * kv:] * row
    pe = jnp.concatenate([e_all[c] for c in range(8)], axis=0)[:, 2 * kv:]
    pec = jnp.concatenate([three, jnp.zeros((128 - kv, 128), F32)], axis=0).T[:2 * kv, :kv]
    xe = early[:, :2 * kv]
    y = hdot(gc, xe, NT)
    xc = factor_inverse(gcc + eye - hdot(y, y, NT))
    xl = -hdot(xc, hdot(y, xe, NN), NN)
    x = jnp.concatenate([
        jnp.concatenate([xe, jnp.zeros((2 * kv, kv), F32)], axis=1),
        jnp.concatenate([xl, xc], axis=1)], axis=0)
    p = jnp.concatenate([
        jnp.concatenate([pe, pec], axis=1),
        jnp.concatenate([pc, pcc], axis=1)], axis=0)
    reduced[...] = hdot(hdot(x, p, NN), x, NT)
    drain(0, e_part, e_in)
    drain(1, l_part, l_in)
    result.wait()


def local(blocks, block_cols, live_counts, onsite_energy, precond, vectors, prev_vectors, prev_image):
    n = lax.axis_size("rows")
    br, slots, bs, _ = blocks.shape
    kv, width = vectors.shape
    nb = 3 * kv
    vmem = pl.BlockSpec(memory_space=pltpu.VMEM)
    smem = pl.BlockSpec(memory_space=pltpu.SMEM)
    hbm = pl.BlockSpec(memory_space=pl.ANY)
    dma = pltpu.SemaphoreType.DMA
    field = pltpu.VMEM((br, kv, bs), F32)
    halo = pltpu.VMEM((HB, kv, bs), F32)
    pair = pltpu.VMEM((br + HB + 1, 3 * kv, bs), BF16)
    moved = pltpu.VMEM((br, slots + 1, kv, bs), F32)
    return pl.pallas_call(
        functools.partial(kernel, n),
        out_shape=(
            jax.ShapeDtypeStruct((kv, width), F32),
            jax.ShapeDtypeStruct((nb, nb), F32),
        ),
        in_specs=[smem, smem, hbm, hbm, hbm, hbm, hbm, hbm],
        out_specs=(hbm, vmem),
        scratch_shapes=[
            pltpu.VMEM((br, bs, slots * bs), BF16),
            pltpu.VMEM((br, bs, slots * bs), E4M3),
            pltpu.VMEM((br, slots * bs, bs), BF16),
            pltpu.VMEM((br, slots * bs, bs), E4M3),
            pltpu.VMEM((br, bs, bs), BF16),
            pltpu.VMEM((br, bs, bs), BF16),
            pltpu.VMEM((RING, slots, bs, bs), F32),
            pltpu.VMEM((br, bs, bs), F32),
            pltpu.VMEM((1, width), F32),
            pltpu.VMEM((kv, width), F32),
            pltpu.VMEM((kv, width), F32),
            pltpu.VMEM((kv, width), F32),
            pltpu.VMEM((kv, width), F32),
            field, field, pair, pair, moved, moved, field, field,
            field, field, field, field, field,
            pltpu.VMEM((4, HB, kv, bs), F32),
            halo, halo,
            pltpu.VMEM((4, HB, kv, bs), F32),
            halo, halo,
            pltpu.VMEM((ROUNDS, 1, 128), F32),
            pltpu.VMEM((ROUNDS, n, 1, 128), F32),
            pltpu.VMEM((8, 8, 128), F32),
            pltpu.VMEM((n, 8, 128), F32),
            pltpu.VMEM((8, 128), F32),
            pltpu.VMEM((8, 8, 128), F32),
            pltpu.VMEM((24, 8, 128), F32),
            pltpu.VMEM((n, 8, 128), F32),
            pltpu.VMEM((8, 128), F32),
            pltpu.VMEM((24, 8, 128), F32),
            pltpu.VMEM((2 * kv, 128), F32),
            dma((br,)),
            dma((4,)),
            dma((4,)),
            dma((1,)),
            dma((5,)),
            dma((5,)),
            dma((5,)),
            dma((5,)),
            dma((ROUNDS,)),
            dma((ROUNDS,)),
            dma((2,)),
            dma((2,)),
            dma((2,)),
            dma((2,)),
        ],
        compiler_params=pltpu.CompilerParams(
            collective_id=0, has_side_effects=True, vmem_limit_bytes=67043328
        ),
    )(block_cols.T, live_counts, blocks, precond, onsite_energy[None, :], vectors, prev_vectors, prev_image)


def solution(mesh):
    placed = (
        P("rows", None, None, None),
        P("rows", None),
        P("rows"),
        P("rows"),
        P("rows", None, None),
        P(None, "rows"),
        P(None, "rows"),
        P(None, "rows"),
    )
    return jax.shard_map(
        local, mesh=mesh, in_specs=placed, out_specs=(P(None, "rows"), P()), check_vma=False
    )
```

time: 107 us -> 64 us (0.60)
  Pallas kernels: 99.7 us -> 58.8 us
  local copies, waits for them, and re-layouts: 4.65 us -> 3.29 us
    pallas_call x1, Pallas kernels: 99.7 us -> 58.8 us  [local(): pl.pallas_call(functools.partial(kernel, n), out_shape=(jax.ShapeDtypeStr...]
    unnamed x3 -> x2, local copies, waits for them, and re-layouts: 4.65 us -> 3.29 us
where the time goes in v1:
time: 64 us; the launch traced here: 62.8 us
  Pallas kernels  58.8 us (92%)
  local copies, waits for them, and re-layouts  3.29 us (5%)
  between operations  0.64 us (1%)
    pallas_call x1, Pallas kernels, local(): pl.pallas_call(functools.partial(kernel, n), out_shape=(jax.ShapeDtypeStr...  58.8 us
    unnamed x2, local copies, waits for them, and re-layouts  3.29 us

profile of v1, /device:TPU:25, one launch (start us, length us, event | category | flops | bytes accessed | tf_op | source)
XLA Modules:
  0.0 62.8 jit_solution(17527508169715044153)
XLA Ops:
  0.6 58.8 %shard_map.95 = (f32[32,4096]{1,0:T(8,128)}, f32[96,96]{1,0:T(8,128)}) custom-call(s32[4,16]{1,0:T(4,128)} %bitcast.3, s32[16]{0:T(128)} %counts.1, f32[16,4,256,256]{3,2,1,0:T(8,128)} %blocks.1, f32[16,256,256]{2,1,0:T(8,128)} %precond.1, f32[1,4096]{1,0:T(1,128)} %bitcast.2, f32[32,4096]{1,0:T(8,128)} %vectors_hbm.1, f32[32,4096]{1,0:T(8,128)} %prev_vectors_hbm.1, ...), custom_call_target="tpu_custom_call" | custom-call | tf_op jit(solution)/shard_map/pallas_call | solution.py:565
  59.5 1.9 %copy.12 = f32[32,4096]{1,0:T(8,128)} copy(f32[32,4096]{1,0:T(8,128)} %get-tuple-element.4) | data formatting | bytes 1048576
  61.3 1.4 %copy.13 = f32[96,96]{1,0:T(8,128)} copy(f32[96,96]{1,0:T(8,128)} %get-tuple-element.5) | data formatting | bytes 73728

commit v2 on v1

--- a/solution.py
+++ b/solution.py
@@ -58,12 +58,13 @@
     correction, reduced,
     w_high, w_low, t_high, t_low, m_high, m_low, stage, pstage,
     onsite, vec, pvec, pimg, cor,
-    field, fieldv, pair, pairv, moved, movedv, fwd, fwdv,
-    image, rem, app, hcorr, srch,
-    halo_in, halov_in, land_out, land_in, landv_out, landv_in,
-    part, sums_in, e_part, e_in, e_sum, e_all, l_part, l_in, l_sum, l_all, early,
+    field, fieldv, pair, pairv, pairp, moved, movedv, movedp, fwd, fwdv, fwdp,
+    image, rem, app, srch, hsrch, hturn,
+    halo_in, halov_in, land_out, land_in, landv_out, landv_in, p_out, p_in, landp_out, landp_in,
+    part, sums_in, x_part, x_in, x_sum, x_all, y_part, y_in, y_sum, y_all,
+    f_part, f_in, early,
     load_sem, pload_sem, in_sem, out_sem, halo_send, halo_recv, land_send, land_recv,
-    sum_send, sum_recv, r_send, r_recv, a_send, a_recv,
+    sum_send, sum_recv, r_send, r_recv, a_send, a_recv, f_send, f_recv,
 ):
     me = lax.axis_index("rows")
     right, left = lax.rem(me + 1, n), lax.rem(me + n - 1, n)
@@ -176,6 +177,7 @@
 
     main = (pair, moved, fwd)
     side = (pairv, movedv, fwdv)
+    rear = (pairp, movedp, fwdp)
 
     def blockloop(lo, hi, body, unroll):
         def step(b, _):
@@ -188,6 +190,17 @@
         high, low = split(x)
         both = dot(jnp.concatenate([high, low], axis=0), m_high[b], NN)
         return both[:kv] + both[kv:] + dot(high, m_low[b], NN)
+
+    def every(lo, hi, body):
+        if hi - lo <= 32:
+            for d in range(lo, hi):
+                body(d)
+        else:
+            def step(d, _):
+                body(d)
+                return 0
+
+            lax.fori_loop(lo, hi, step, 0)
 
     def sum_copy(k, d):
         return pltpu.make_async_remote_copy(
@@ -207,11 +220,7 @@
         part[k] = mine
         sums_in[k, me] = mine
 
-        def send(d, _):
-            sum_copy(k, d).start()
-            return 0
-
-        lax.fori_loop(1, n, send, 0)
+        every(1, n, lambda d: sum_copy(k, d).start())
 
     def bulk(ref, sem):
         return pltpu.make_async_copy(ref, ref, sem)
@@ -227,20 +236,20 @@
     def scatter(r, sheet, held, landed):
         chunks = held.shape[0]
         for c in range(chunks):
-            held[c] = sheet[c]
-
-        def send(d, _):
-            to = lax.rem(me + d, n)
-
-            @pl.when(to < chunks)
+            if sheet[c] is not None:
+                held[c] = sheet[c]
+
+        def send(d):
+            to = lax.rem(me + d, chunks)
+
+            @pl.when(to != me)
             def _():
                 pltpu.make_async_remote_copy(
-                    src_ref=held.at[jnp.minimum(to, chunks - 1)], dst_ref=landed.at[me],
+                    src_ref=held.at[to], dst_ref=landed.at[me],
                     send_sem=r_send.at[r], recv_sem=r_recv.at[r],
                     device_id=(to,), device_id_type=MESH).start()
-            return 0
-
-        lax.fori_loop(1, n, send, 0)
+
+        every(0, chunks, send)
 
     def spread_sums(r, held, landed, mine, everything):
         chunks = held.shape[0]
@@ -253,14 +262,13 @@
             mine[...] = whole
             everything[jnp.minimum(me, chunks - 1)] = whole
 
-            def send(d, _):
+            def send(d):
                 pltpu.make_async_remote_copy(
                     src_ref=mine, dst_ref=everything.at[jnp.minimum(me, chunks - 1)],
                     send_sem=a_send.at[r], recv_sem=a_recv.at[r],
                     device_id=(lax.rem(me + d, n),), device_id_type=MESH).start()
-                return 0
-
-            lax.fori_loop(1, n, send, 0)
+
+            every(1, n, send)
 
     def collect(r, held, landed, everything):
         chunks = held.shape[0]
@@ -289,8 +297,10 @@
     for c in range(br):
         moved[c, slots] = zero
         movedv[c, slots] = zero
+        movedp[c, slots] = zero
     pair[br + HB] = jnp.zeros((3 * kv, bs), BF16)
     pairv[br + HB] = jnp.zeros((3 * kv, bs), BF16)
+    pairp[br + HB] = jnp.zeros((3 * kv, bs), BF16)
     inputs[0].wait()
     for b in range(br):
         x = vec[:, lanes(b)]
@@ -358,41 +368,31 @@
         halo.wait_recv()
         for i in range(HB):
             put(pair, br + i, halo_in[k, i])
-        if more:
-            more[0].wait_recv()
+        for group, copies, arrived in more:
+            copies[0].wait_recv()
             for i in range(HB):
-                put(pairv, br + i, halov_in[i])
+                put(group[0], br + i, arrived[i])
         for b in range(first, br):
             forward(b, groups)
         land.wait_recv()
-        if more:
-            more[1].wait_recv()
-        for copy in (halo, land) + tuple(more):
-            copy.wait_send()
-
-    def applied(k, group, landed, held, b):
-        got = group[2][b] + landing(group, b) + onsite[:, lanes(b)] * held[b]
-        return got + landed(b) if b < HB else got
-
-    def middle(k, update, groups):
-        sums = [zero, zero]
-
-        def one(b):
-            out, a, c = update(b)
-            sums[0] = sums[0] + a
-            sums[1] = sums[1] + c
-            return out
-
+        for group, copies, arrived in more:
+            copies[1].wait_recv()
+            copies[0].wait_send()
+            copies[1].wait_send()
+        halo.wait_send()
+        land.wait_send()
+
+    def begin(k, update, outs_to, groups):
         def pre(b, x):
             y = precondition(b, x)
-            field[b] = y
+            outs_to[b] = y
             put(pair, b, y)
 
         for b in range(HB):
-            pre(b, one(b))
-        halo = halo_copy(k, field, halo_in.at[k])
+            pre(b, update(b))
+        halo = halo_copy(k, outs_to, halo_in.at[k])
         halo.start()
-        outs = [one(b) for b in range(first, br)]
+        outs = [update(b) for b in range(first, br)]
         for b in range(first, br):
             pre(b, outs[b - first])
         for b in range(first, br):
@@ -401,15 +401,47 @@
             land_out[i] = landing(main, br + i)
         land = land_copy(k, land_out, land_in.at[k])
         land.start()
-        outs = [one(b) for b in range(HB, first)]
-        sum_start(k - 1, *sums)
-        for b in range(HB, first):
-            pre(b, outs[b - HB])
-        blockloop(0, first, lambda b: spread(b, groups), 4)
-        blockloop(0, first, lambda b: forward(b, groups), 4)
-        return halo, land
+        outs = [update(b) for b in range(HB, first)]
+
+        def rest():
+            for b in range(HB, first):
+                pre(b, outs[b - HB])
+
+        return halo, land, rest
+
+    def middle(groups):
+        def both_ways(b):
+            spread(b, groups)
+            forward(b, groups)
+
+        blockloop(0, first, both_ways, 4)
+
+    def totals():
+        sums = [zero, zero]
+
+        def add(a, c):
+            sums[0] = sums[0] + a
+            sums[1] = sums[1] + c
+
+        return sums, add
+
+    def gram(lhs, rhs):
+        got = None
+        for b in range(br):
+            lh, ll = split(jnp.concatenate(lhs(b), axis=0))
+            rh, rl = split(jnp.concatenate(rhs(b), axis=0))
+            m = lh.shape[0]
+            both = dot(jnp.concatenate([lh, ll], axis=0), rh, NT)
+            one = both[:m] + both[m:] + dot(lh, rl, NT)
+            got = one if got is None else got + one
+        return got
+
+    def rows8(sheets):
+        return [s[c * 8:(c + 1) * 8] for s in sheets for c in range(s.shape[0] // 8)]
 
     finish(0, [main], halo, land, ())
+
+    sums, add = totals()
 
     def after0(b):
         x = vec[:, lanes(b)]
@@ -417,22 +449,37 @@
         if b < HB:
             got = got + land_in[0, b]
         image[b] = got
-        return got, x * got, x * x
-
-    halo, land = middle(1, after0, [main, side])
+        add(x * got, x * x)
+        return got
+
+    halo, land, rest = begin(1, after0, field, [main])
+    sum_start(0, *sums)
+    rest()
+    middle([main, side])
     inputs[2].wait()
     inputs[3].wait()
-    both = jnp.zeros((2 * kv, 4 * kv), F32)
     for b in range(br):
-        basis = jnp.concatenate([vec[:, lanes(b)], pvec[:, lanes(b)]], axis=0)
-        other = jnp.concatenate([basis, image[b], pimg[:, lanes(b)]], axis=0)
-        oh, ol = split(other)
-        bh, bl = oh[:2 * kv], ol[:2 * kv]
-        both = both + dot(bh, oh, NT) + dot(bl, oh, NT) + dot(bh, ol, NT)
-    scatter(0, [both[c * 8:(c + 1) * 8] for c in range(8)], e_part, e_in)
-    finish(1, [main, side], halo, land, (halov, landv))
+        x = pvec[:, lanes(b)]
+        put(pairp, b, x)
+        if b < HB:
+            p_out[b] = x
+    halop = halo_copy(5, p_out, p_in)
+    halop.start()
+    for b in range(first, br):
+        spread(b, [rear])
+    for i in range(HB):
+        landp_out[i] = landing(rear, br + i)
+    landp = land_copy(5, landp_out, landp_in)
+    landp.start()
+    both = gram(lambda b: [vec[:, lanes(b)], pvec[:, lanes(b)]],
+                lambda b: [vec[:, lanes(b)], pvec[:, lanes(b)], image[b], pimg[:, lanes(b)]])
+    for c, rows in enumerate(rows8([both])):
+        x_part[c] = rows
+    finish(1, [main, side], halo, land, [(side, (halov, landv), halov_in)])
     numerator, denominator = sum_finish(0)
     quotient = numerator / denominator
+
+    sums, add = totals()
 
     def after1(b):
         xv, xi = fieldv[b], field[b]
@@ -443,39 +490,95 @@
             hv = hv + landv_in[b]
             hi = hi + land_in[1, b]
         x = quotient * xv - xi
+        h = quotient * hv - hi
         r = quotient * vec[:, lanes(b)] - image[b]
-        a = quotient * hv - hi - quotient * x
+        a = h - quotient * x
         srch[b] = x
+        hsrch[b] = h
         rem[b] = r
         app[b] = a
-        return a, a * r, a * a
-
-    halo, land = middle(2, after1, [main])
-    spread_sums(0, e_part, e_in, e_sum, e_all)
-    finish(2, [main], halo, land, ())
+        add(a * r, a * a)
+        return a
+
+    halo, land, rest = begin(2, after1, field, [main])
+    sum_start(1, *sums)
+    rest()
+    middle([main, rear])
+    both = gram(lambda b: [srch[b], field[b]],
+                lambda b: [vec[:, lanes(b)], pvec[:, lanes(b)], srch[b], field[b],
+                           image[b], pimg[:, lanes(b)], hsrch[b], hsrch[b]])
+    scatter(0, [None] * 8 + rows8([both[:, :128], both[:, 128:]]), x_part, x_in)
+    finish(2, [main, rear], halo, land, [(rear, (halop, landp), p_in)])
+
+    def after2(b):
+        t = field[b]
+        got = fwd[b] + landing(main, b) + onsite[:, lanes(b)] * t
+        if b < HB:
+            got = got + land_in[2, b]
+        hturn[b] = got
+        return got - quotient * t
+
+    halo, land, rest = begin(3, after2, fieldv, [main])
     step = sum_finish(1)
-    step = step[0] / (step[1] + 1.0)
-
-    def advance_step(k, start, b):
-        x, y, t = srch[b], app[b], field[b]
-        on = onsite[:, lanes(b)]
-        g = fwd[b] + landing(main, b) + (on - quotient) * t
+    step1 = step[0] / (step[1] + 1.0)
+    sums, add = totals()
+    for b in range(br):
+        r = rem[b] - step1 * app[b]
+        a = app[b] - step1 * (hturn[b] - quotient * field[b])
+        rem[b] = r
+        app[b] = a
+        add(a * r, a * a)
+    sum_start(2, *sums)
+    rest()
+    for b in range(br):
+        got = fwdp[b] + landing(rear, b) + onsite[:, lanes(b)] * pvec[:, lanes(b)]
+        fwdp[b] = got + landp_in[b] if b < HB else got
+    one = gram(lambda b: [fieldv[b]],
+               lambda b: [vec[:, lanes(b)], pvec[:, lanes(b)], srch[b], field[b],
+                          image[b], pimg[:, lanes(b)], hsrch[b], fieldv[b]])
+    two = gram(lambda b: [fieldv[b], srch[b], field[b]], lambda b: [fwdp[b], hturn[b]])
+    three = jnp.concatenate([two[:kv], two[2 * kv:]], axis=1)
+    four = jnp.concatenate([two[kv:2 * kv], two[kv:2 * kv]], axis=1)
+    scatter(1, rows8([one[:, :128], one[:, 128:], three, four]), y_part, y_in)
+    middle([main])
+    spread_sums(0, x_part, x_in, x_sum, x_all)
+    finish(3, [main], halo, land, ())
+    step = sum_finish(2)
+    step2 = step[0] / (step[1] + 1.0)
+
+    sums, add = totals()
+    for b in range(br):
+        u = fieldv[b]
+        got = fwd[b] + landing(main, b) + onsite[:, lanes(b)] * u
         if b < HB:
-            g = g + land_in[k, b]
-        c = step * x
-        h = step * (y + quotient * x)
-        cor[:, lanes(b)] = c if start else cor[:, lanes(b)] + c
-        hcorr[b] = h if start else hcorr[b] + h
-        r = rem[b] - step * y
-        z = y - step * g
-        srch[b] = x - step * t
-        rem[b] = r
-        app[b] = z
-        return z, z * r, z * z
-
-    halo, land = middle(3, lambda b: advance_step(2, True, b), [main])
-    collect(0, e_part, e_in, e_all)
-    known = jnp.concatenate([e_all[c] for c in range(8)], axis=0)
+            got = got + land_in[3, b]
+        image[b] = got
+        a = app[b]
+        r = rem[b] - step2 * a
+        g = hturn[b] - quotient * field[b]
+        a = a - step2 * (g - step1 * (got - quotient * u))
+        add(a * r, a * a)
+    square = gram(lambda b: [fieldv[b]], lambda b: [image[b]])
+    flat = jnp.concatenate([square[8 * c:8 * c + 8] for c in range(4)], axis=1)
+    wide = jnp.broadcast_to(lane_sums(*sums), (2 * kv, 128))
+    wide = jnp.concatenate([wide, jnp.zeros((128 - 2 * kv, 128), F32)], axis=0)
+    f_part[8] = wide.T[:1]
+    for i in range(8):
+        f_part[i] = flat[i:i + 1]
+    f_in[me] = f_part[...]
+
+    def last_send(d):
+        pltpu.make_async_remote_copy(
+            src_ref=f_part, dst_ref=f_in.at[me],
+            send_sem=f_send.at[0], recv_sem=f_recv.at[0],
+            device_id=(lax.rem(me + d, n),), device_id_type=MESH).start()
+
+    every(1, n, last_send)
+
+    spread_sums(1, y_part, y_in, y_sum, y_all)
+
+    collect(0, x_part, x_in, x_all)
+    known = jnp.concatenate([x_all[c] for c in range(8)], axis=0)
     rows_at = lax.broadcasted_iota(jnp.int32, (kv, kv), 0)
     eye = jnp.where(rows_at == lax.broadcasted_iota(jnp.int32, (kv, kv), 1), 1.0, 0.0).astype(F32)
     x11 = factor_inverse(known[:kv, :kv] + eye)
@@ -484,55 +587,49 @@
     x21 = -hdot(x22, hdot(y21, x11, NN), NN)
     early[0:kv] = jnp.concatenate([x11, jnp.zeros((kv, 128 - kv), F32)], axis=1)
     early[kv:2 * kv] = jnp.concatenate([x21, x22, jnp.zeros((kv, 128 - 2 * kv), F32)], axis=1)
-    finish(3, [main], halo, land, ())
-    step = sum_finish(2)
-    step = step[0] / (step[1] + 1.0)
-
-    sums = [zero, zero]
-    both = jnp.zeros((4 * kv, 8 * kv), F32)
+    collect(1, y_part, y_in, y_all)
+
+    def sheet(held, i, count):
+        return jnp.concatenate([held[i * count + c] for c in range(count)], axis=0)
+
+    def turned(t):
+        return jnp.concatenate([t, jnp.zeros((128 - kv, 128), F32)], axis=0).T[:, :kv]
+
+    xg, xh = sheet(x_all, 1, 8), sheet(x_all, 2, 8)
+    ug, uh, third, fourth = [sheet(y_all, i, 4) for i in range(4)]
+    ug_t, uh_t, third_t = turned(ug), turned(uh), turned(third)
+    bulk(f_in.at[pl.ds(0, n - 1)], f_recv.at[0]).wait()
+    whole = jnp.sum(f_in[...], axis=0)
+    bulk(f_in.at[pl.ds(0, n - 1)], f_send.at[0]).wait()
+    flat = jnp.concatenate([whole[i] for i in range(8)], axis=0)
+    uhu = jnp.concatenate([flat[:, kv * c:kv * c + kv] for c in range(4)], axis=0)
+    column = jnp.broadcast_to(whole[8], (128, 128)).T
+    step3 = column[:kv] / (column[kv:2 * kv] + 1.0)
+    step1, step2 = step1[:, :128], step2[:, :128]
+    ca = step1 + step2 + step3
+    ct = -(step1 * step2 + step3 * (step1 + step2))
+    cu = step1 * step2 * step3
+    wa, wt, wu = [jnp.concatenate([c, c], axis=1) for c in (ca, ct, cu)]
     for b in range(br):
-        z, one, two = advance_step(3, False, b)
-        sums = [sums[0] + one, sums[1] + two]
-        x = srch[b]
-        mine = cor[:, lanes(b)]
-        hmine = hcorr[b]
-        w = z + quotient * x
-        ch, cl = split(jnp.concatenate([mine, x], axis=0))
-        hh, hl = split(jnp.concatenate([hmine, w], axis=0))
-        vh, vl = split(jnp.concatenate([vec[:, lanes(b)], pvec[:, lanes(b)]], axis=0))
-        ih, il = split(jnp.concatenate([image[b], pimg[:, lanes(b)]], axis=0))
-        lh = jnp.concatenate([ch, hh], axis=0)
-        ll = jnp.concatenate([cl, hl], axis=0)
-        oh = jnp.concatenate([vh, ch, ih, hh], axis=0)
-        ol = jnp.concatenate([vl, cl, il, hl], axis=0)
-        both = both + dot(lh, oh, NT) + dot(ll, oh, NT) + dot(lh, ol, NT)
-    lane_at = lax.broadcasted_iota(jnp.int32, (2 * kv, 128), 1)
-    third = jnp.where(
-        lane_at < 2 * kv, both[2 * kv:, :128], jnp.broadcast_to(lane_sums(*sums), (2 * kv, 128)))
-    sheets = [both[:2 * kv, :128], both[:2 * kv, 128:], third]
-    scatter(1, [s[c * 8:(c + 1) * 8] for s in sheets for c in range(8)], l_part, l_in)
-    spread_sums(1, l_part, l_in, l_sum, l_all)
-    collect(1, l_part, l_in, l_all)
-    one, two, three = [
-        jnp.concatenate([l_all[8 * i + c] for c in range(8)], axis=0) for i in range(3)]
-    cross = jnp.broadcast_to(three[:kv, 2 * kv:2 * kv + 1], (kv, 128))
-    own = jnp.broadcast_to(three[kv:, 2 * kv:2 * kv + 1], (kv, 128))
-    step = cross / (own + 1.0)
-    wide = jnp.concatenate([step, step], axis=1)
-    for b in range(br):
-        cor[:, lanes(b)] = cor[:, lanes(b)] + wide * srch[b]
+        cor[:, lanes(b)] = wa * srch[b] + wt * field[b] + wu * fieldv[b]
     result = pltpu.make_async_copy(cor, correction, out_sem.at[0])
     result.start()
-    row = jnp.concatenate([step, jnp.zeros((128 - kv, 128), F32)], axis=0).T[:kv, :kv]
-    one = one[:kv] + step * one[kv:]
-    two = two[:kv] + step * two[kv:]
-    three = three[:kv] + step * three[kv:]
-    gc = one[:, :2 * kv]
-    gcc = one[:, 2 * kv:3 * kv] + one[:, 3 * kv:] * row
-    pc = two[:, :2 * kv]
-    pcc = two[:, 2 * kv:3 * kv] + two[:, 3 * kv:] * row
-    pe = jnp.concatenate([e_all[c] for c in range(8)], axis=0)[:, 2 * kv:]
-    pec = jnp.concatenate([three, jnp.zeros((128 - kv, 128), F32)], axis=0).T[:2 * kv, :kv]
+    row = jnp.concatenate([ca, ct, cu, jnp.zeros((128 - 3 * kv, 128), F32)], axis=0).T
+    ra, rt, ru = [row[:kv, kv * i:kv * i + kv] for i in range(3)]
+    g = ca * xg[:kv] + ct * xg[kv:] + cu * ug
+    h = ca * xh[:kv] + ct * xh[kv:] + cu * uh
+    na, nt, nu = ca[:, :kv], ct[:, :kv], cu[:, :kv]
+    gu = na * ug_t[2 * kv:3 * kv] + nt * ug_t[3 * kv:] + nu * uh[:, 3 * kv:]
+    gc = g[:, :2 * kv]
+    gcc = g[:, 2 * kv:3 * kv] * ra + g[:, 3 * kv:] * rt + gu * ru
+    pc = h[:, :2 * kv]
+    both = ca * jnp.concatenate([fourth[:, :2 * kv], fourth[:, :2 * kv]], axis=1) + cu * third
+    chp = both[:, :kv] + nt * third[:, 2 * kv:3 * kv]
+    cht = both[:, kv:2 * kv] + nt * third[:, 3 * kv:]
+    chu = na * uh_t[2 * kv:3 * kv] + nt * third_t[kv:2 * kv] + nu * uhu
+    pcc = h[:, 2 * kv:3 * kv] * ra + cht * rt + chu * ru
+    pec = turned(jnp.concatenate([h[:, :kv], chp, jnp.zeros((kv, 128 - 2 * kv), F32)], axis=1))[:2 * kv]
+    pe = sheet(x_all, 0, 8)[:, 2 * kv:]
     xe = early[:, :2 * kv]
     y = hdot(gc, xe, NT)
     xc = factor_inverse(gcc + eye - hdot(y, y, NT))
@@ -544,8 +641,8 @@
         jnp.concatenate([pe, pec], axis=1),
         jnp.concatenate([pc, pcc], axis=1)], axis=0)
     reduced[...] = hdot(hdot(x, p, NN), x, NT)
-    drain(0, e_part, e_in)
-    drain(1, l_part, l_in)
+    drain(0, x_part, x_in)
+    drain(1, y_part, y_in)
     result.wait()
 
 
@@ -562,6 +659,11 @@
     halo = pltpu.VMEM((HB, kv, bs), F32)
     pair = pltpu.VMEM((br + HB + 1, 3 * kv, bs), BF16)
     moved = pltpu.VMEM((br, slots + 1, kv, bs), F32)
+
+    def reduction(chunks):
+        tiles = [(chunks, 8, 128), (n, 8, 128), (8, 128), (chunks, 8, 128)]
+        return [pltpu.VMEM(t, F32) for t in tiles]
+
     return pl.pallas_call(
         functools.partial(kernel, n),
         out_shape=(
@@ -584,37 +686,34 @@
             pltpu.VMEM((kv, width), F32),
             pltpu.VMEM((kv, width), F32),
             pltpu.VMEM((kv, width), F32),
-            field, field, pair, pair, moved, moved, field, field,
-            field, field, field, field, field,
+            field, field, pair, pair, pair, moved, moved, moved, field, field, field,
+            field, field, field, field, field, field,
             pltpu.VMEM((4, HB, kv, bs), F32),
             halo, halo,
             pltpu.VMEM((4, HB, kv, bs), F32),
-            halo, halo,
+            halo, halo, halo, halo, halo, halo,
             pltpu.VMEM((ROUNDS, 1, 128), F32),
             pltpu.VMEM((ROUNDS, n, 1, 128), F32),
-            pltpu.VMEM((8, 8, 128), F32),
-            pltpu.VMEM((n, 8, 128), F32),
-            pltpu.VMEM((8, 128), F32),
-            pltpu.VMEM((8, 8, 128), F32),
-            pltpu.VMEM((24, 8, 128), F32),
-            pltpu.VMEM((n, 8, 128), F32),
-            pltpu.VMEM((8, 128), F32),
-            pltpu.VMEM((24, 8, 128), F32),
+            *reduction(24), *reduction(16),
+            pltpu.VMEM((9, 1, 128), F32),
+            pltpu.VMEM((n, 9, 1, 128), F32),
             pltpu.VMEM((2 * kv, 128), F32),
             dma((br,)),
             dma((4,)),
             dma((4,)),
             dma((1,)),
-            dma((5,)),
-            dma((5,)),
-            dma((5,)),
-            dma((5,)),
+            dma((6,)),
+            dma((6,)),
+            dma((6,)),
+            dma((6,)),
             dma((ROUNDS,)),
             dma((ROUNDS,)),
             dma((2,)),
             dma((2,)),
             dma((2,)),
             dma((2,)),
+            dma((1,)),
+            dma((1,)),
         ],
         compiler_params=pltpu.CompilerParams(
             collective_id=0, has_side_effects=True, vmem_limit_bytes=67043328

time: 64 us -> 60 us (0.938); the launches traced: 62.8 us -> 59.7 us
  Pallas kernels: 58.8 us -> 55.8 us
    pallas_call x1, Pallas kernels: 58.8 us -> 55.8 us  [local(): pl.pallas_call(functools.partial(kernel, n), out_shape=(jax.ShapeDtypeStr...]
where the time goes in v2:
time: 60 us; the launch traced here: 59.7 us
  Pallas kernels  55.8 us (93%)
  local copies, waits for them, and re-layouts  3.29 us (5%)
  between operations  0.64 us (1%)
    pallas_call x1, Pallas kernels, local(): pl.pallas_call(functools.partial(kernel, n), out_shape=(jax.ShapeDtypeStr...  55.8 us
    unnamed x2, local copies, waits for them, and re-layouts  3.29 us

profile of v2, /device:TPU:25, one launch (start us, length us, event | category | flops | bytes accessed | tf_op | source)
XLA Modules:
  0.0 59.7 jit_solution(4316800318589040409)
XLA Ops:
  0.6 55.8 %shard_map.95 = (f32[32,4096]{1,0:T(8,128)}, f32[96,96]{1,0:T(8,128)}) custom-call(s32[4,16]{1,0:T(4,128)} %bitcast.3, s32[16]{0:T(128)} %counts.1, f32[16,4,256,256]{3,2,1,0:T(8,128)} %blocks.1, f32[16,256,256]{2,1,0:T(8,128)} %precond.1, f32[1,4096]{1,0:T(1,128)} %bitcast.2, f32[32,4096]{1,0:T(8,128)} %vectors_hbm.1, f32[32,4096]{1,0:T(8,128)} %prev_vectors_hbm.1, ...), custom_call_target="tpu_custom_call" | custom-call | tf_op jit(solution)/shard_map/pallas_call | solution.py:667
  56.4 1.9 %copy.12 = f32[32,4096]{1,0:T(8,128)} copy(f32[32,4096]{1,0:T(8,128)} %get-tuple-element.4) | data formatting | bytes 1048576
  58.3 1.4 %copy.13 = f32[96,96]{1,0:T(8,128)} copy(f32[96,96]{1,0:T(8,128)} %get-tuple-element.5) | data formatting | bytes 73728

commit v3 on v2

--- a/solution.py
+++ b/solution.py
@@ -96,6 +96,10 @@
     inputs[1].start()
     for t in range(RING):
         load(t).start()
+    for c in range(4):
+        pload(c).start()
+    inputs[2].start()
+    inputs[3].start()
 
     def greet(d, _):
         pl.semaphore_signal(barrier, inc=1, device_id=(lax.rem(me + d, n),), device_id_type=MESH)
@@ -310,18 +314,15 @@
 
     def advance(t):
         load(t).wait()
-        take_tiles(t)
-        if t + RING < br:
-            load(t + RING).start()
-        elif t + RING == br:
-            for c in range(4):
-                pload(c).start()
-            inputs[2].start()
-            inputs[3].start()
+        if t and t - 1 + RING < br:
+            load(t - 1 + RING).start()
 
     for t in range(HB):
         advance(t)
-        spread(order[t], [main])
+        if t:
+            spread(order[t - 1], [main])
+        take_tiles(t)
+    spread(order[HB - 1], [main])
     for i in range(HB):
         land_out[i] = landing(main, br + i)
     pl.semaphore_wait(barrier, n - 1)
@@ -331,11 +332,12 @@
     land.start()
     for t in range(HB, br):
         advance(t)
-        spread(order[t], [main])
-        if t - HB >= HB:
-            forward(t - 2 * HB, [main])
-    for b in range(first - HB, first):
-        forward(b, [main])
+        if t > HB:
+            spread(order[t - 1], [main])
+            forward(order[t - 1], [main])
+        take_tiles(t)
+    spread(first - 1, [main])
+    forward(first - 1, [main])
 
     for c in range(4):
         pload(c).wait()
@@ -543,6 +545,7 @@
     middle([main])
     spread_sums(0, x_part, x_in, x_sum, x_all)
     finish(3, [main], halo, land, ())
+    spread_sums(1, y_part, y_in, y_sum, y_all)
     step = sum_finish(2)
     step2 = step[0] / (step[1] + 1.0)
 
@@ -575,7 +578,6 @@
 
     every(1, n, last_send)
 
-    spread_sums(1, y_part, y_in, y_sum, y_all)
 
     collect(0, x_part, x_in, x_all)
     known = jnp.concatenate([x_all[c] for c in range(8)], axis=0)
@@ -633,14 +635,19 @@
     xe = early[:, :2 * kv]
     y = hdot(gc, xe, NT)
     xc = factor_inverse(gcc + eye - hdot(y, y, NT))
-    xl = -hdot(xc, hdot(y, xe, NN), NN)
     x = jnp.concatenate([
         jnp.concatenate([xe, jnp.zeros((2 * kv, kv), F32)], axis=1),
-        jnp.concatenate([xl, xc], axis=1)], axis=0)
+        jnp.concatenate([-hdot(y, xe, NN), eye], axis=1)], axis=0)
     p = jnp.concatenate([
         jnp.concatenate([pe, pec], axis=1),
         jnp.concatenate([pc, pcc], axis=1)], axis=0)
-    reduced[...] = hdot(hdot(x, p, NN), x, NT)
+    q = hdot(hdot(x, p, NN), x, NT)
+    edge = lax.broadcasted_iota(jnp.int32, (2 * kv, 3 * kv), 0) == lax.broadcasted_iota(
+        jnp.int32, (2 * kv, 3 * kv), 1)
+    d = jnp.concatenate([
+        jnp.where(edge, 1.0, 0.0).astype(F32),
+        jnp.concatenate([jnp.zeros((kv, 2 * kv), F32), xc], axis=1)], axis=0)
+    reduced[...] = hdot(hdot(d, q, NN), d, NT)
     drain(0, x_part, x_in)
     drain(1, y_part, y_in)
     result.wait()

time: 60 us -> 59 us (0.983)
  Pallas kernels: 55.8 us -> 54.8 us
    pallas_call x1, Pallas kernels: 55.8 us -> 54.8 us  [local(): pl.pallas_call(functools.partial(kernel, n), out_shape=(jax.ShapeDtypeStr...]
where the time goes in v3:
time: 59 us; the launch traced here: 58.7 us
  Pallas kernels  54.8 us (93%)
  local copies, waits for them, and re-layouts  3.29 us (6%)
  between operations  0.64 us (1%)
    pallas_call x1, Pallas kernels, local(): pl.pallas_call(functools.partial(kernel, n), out_shape=(jax.ShapeDtypeStr...  54.8 us
    unnamed x2, local copies, waits for them, and re-layouts  3.29 us

profile of v3, /device:TPU:25, one launch (start us, length us, event | category | flops | bytes accessed | tf_op | source)
XLA Modules:
  0.0 58.7 jit_solution(1681163993301585456)
XLA Ops:
  0.6 54.8 %shard_map.95 = (f32[32,4096]{1,0:T(8,128)}, f32[96,96]{1,0:T(8,128)}) custom-call(s32[4,16]{1,0:T(4,128)} %bitcast.3, s32[16]{0:T(128)} %counts.1, f32[16,4,256,256]{3,2,1,0:T(8,128)} %blocks.1, f32[16,256,256]{2,1,0:T(8,128)} %precond.1, f32[1,4096]{1,0:T(1,128)} %bitcast.2, f32[32,4096]{1,0:T(8,128)} %vectors_hbm.1, f32[32,4096]{1,0:T(8,128)} %prev_vectors_hbm.1, ...), custom_call_target="tpu_custom_call" | custom-call | tf_op jit(solution)/shard_map/pallas_call | solution.py:674
  55.4 1.9 %copy.12 = f32[32,4096]{1,0:T(8,128)} copy(f32[32,4096]{1,0:T(8,128)} %get-tuple-element.4) | data formatting | bytes 1048576
  57.3 1.4 %copy.13 = f32[96,96]{1,0:T(8,128)} copy(f32[96,96]{1,0:T(8,128)} %get-tuple-element.5) | data formatting | bytes 73728

commit v4 on v3

--- a/solution.py
+++ b/solution.py
@@ -384,7 +384,7 @@
         halo.wait_send()
         land.wait_send()
 
-    def begin(k, update, outs_to, groups):
+    def begin(k, update, outs_to, send_sums):
         def pre(b, x):
             y = precondition(b, x)
             outs_to[b] = y
@@ -397,13 +397,14 @@
         outs = [update(b) for b in range(first, br)]
         for b in range(first, br):
             pre(b, outs[b - first])
+        outs = [update(b) for b in range(HB, first)]
+        send_sums()
         for b in range(first, br):
             spread(b, [main])
         for i in range(HB):
             land_out[i] = landing(main, br + i)
         land = land_copy(k, land_out, land_in.at[k])
         land.start()
-        outs = [update(b) for b in range(HB, first)]
 
         def rest():
             for b in range(HB, first):
@@ -454,8 +455,7 @@
         add(x * got, x * x)
         return got
 
-    halo, land, rest = begin(1, after0, field, [main])
-    sum_start(0, *sums)
+    halo, land, rest = begin(1, after0, field, lambda: sum_start(0, *sums))
     rest()
     middle([main, side])
     inputs[2].wait()
@@ -502,8 +502,7 @@
         add(a * r, a * a)
         return a
 
-    halo, land, rest = begin(2, after1, field, [main])
-    sum_start(1, *sums)
+    halo, land, rest = begin(2, after1, field, lambda: sum_start(1, *sums))
     rest()
     middle([main, rear])
     both = gram(lambda b: [srch[b], field[b]],
@@ -520,7 +519,7 @@
         hturn[b] = got
         return got - quotient * t
 
-    halo, land, rest = begin(3, after2, fieldv, [main])
+    halo, land, rest = begin(3, after2, fieldv, lambda: None)
     step = sum_finish(1)
     step1 = step[0] / (step[1] + 1.0)
     sums, add = totals()

time: 59 us -> 59.1 us (level)
  no operation moved by 1% of the time
where the time goes in v4:
time: 59.1 us; the launch traced here: 58.8 us
  Pallas kernels  54.9 us (93%)
  local copies, waits for them, and re-layouts  3.29 us (6%)
  between operations  0.64 us (1%)
    pallas_call x1, Pallas kernels, local(): pl.pallas_call(functools.partial(kernel, n), out_shape=(jax.ShapeDtypeStr...  54.9 us
    unnamed x2, local copies, waits for them, and re-layouts  3.29 us

profile of v4, /device:TPU:25, one launch (start us, length us, event | category | flops | bytes accessed | tf_op | source)
XLA Modules:
  0.0 58.8 jit_solution(11551043905588416068)
XLA Ops:
  0.6 54.9 %shard_map.95 = (f32[32,4096]{1,0:T(8,128)}, f32[96,96]{1,0:T(8,128)}) custom-call(s32[4,16]{1,0:T(4,128)} %bitcast.3, s32[16]{0:T(128)} %counts.1, f32[16,4,256,256]{3,2,1,0:T(8,128)} %blocks.1, f32[16,256,256]{2,1,0:T(8,128)} %precond.1, f32[1,4096]{1,0:T(1,128)} %bitcast.2, f32[32,4096]{1,0:T(8,128)} %vectors_hbm.1, f32[32,4096]{1,0:T(8,128)} %prev_vectors_hbm.1, ...), custom_call_target="tpu_custom_call" | custom-call | tf_op jit(solution)/shard_map/pallas_call | solution.py:673
  55.6 1.9 %copy.12 = f32[32,4096]{1,0:T(8,128)} copy(f32[32,4096]{1,0:T(8,128)} %get-tuple-element.4) | data formatting | bytes 1048576
  57.4 1.4 %copy.13 = f32[96,96]{1,0:T(8,128)} copy(f32[96,96]{1,0:T(8,128)} %get-tuple-element.5) | data formatting | bytes 73728
